TPU v7x, 32 devices: a whole 2x2x4 slice. The times are simulated.
32 devices in a mesh: grp: 2 (over x), tok: 8 (over z, y), side: 2 (over core).
Axes of the slice: x: 2, y: 2, z: 4, core: 2. Of those that a mesh axis runs over, the one named last changes fastest.
Arguments:
- hidden_in: bfloat16 [512, 3072], P(('grp', 'tok')), parts along dimension 0, may hold values from -6 to 6
- queries: bfloat16 [512, 24, 128], P(('grp', 'tok'), 'side'), parts along dimension 0, may hold values from -32 to 32
- key_new: bfloat16 [512, 4, 128], P(('grp', 'tok'), 'side'), parts along dimension 0, may hold values from -32 to 32
- value_new: bfloat16 [512, 4, 128], P(('grp', 'tok'), 'side'), parts along dimension 0, may hold values from -6 to 6
- cache_keys: bfloat16 [512, 4, 128, 128], P(('grp', 'tok'), 'side'), parts along dimension 0, may hold values from -32 to 32
- cache_values: bfloat16 [512, 4, 128, 128], P(('grp', 'tok'), 'side'), parts along dimension 0, may hold values from -6 to 6
- lengths: int32 [512], P(('grp', 'tok')), parts along dimension 0, may hold values from 1 to 128, 16384 in all
- out_weight: bfloat16 [3072, 3072], P('side', 'tok'), may hold values from -0.109375 to 0.109375
- norm_gain: float32 [3072], replicated, may hold values from 0.1 to 1.9
- router_weight: float32 [3072, 4], replicated, may hold values from -0.109375 to 0.109375
- gate_weight: bfloat16 [3072, 32768], P(None, ('tok', 'side')), may hold values from -0.109375 to 0.109375
- up_weight: bfloat16 [3072, 32768], P(None, ('tok', 'side')), may hold values from -0.109375 to 0.109375
- down_weight: bfloat16 [32768, 3072], P(('tok', 'side')), may hold values from -0.0625 to 0.0625
- routes: int32 [512, 2], P('grp'), parts along dimension 0, may hold values from 0 to 3, all different within a row; in each aligned block of 32 rows (0 to 31, 32 to 63, ...) at most 24 rows name the same one
Outputs:
- mixed: bfloat16 [512, 3072], P(('grp', 'tok')), parts along dimension 0
There are 2 independent parts, one for each index of `grp`. A program takes and returns all parts, laid end to end along the dimension named above; an argument that names none is the same for every part. Nothing has to cross between parts.
Inputs may be any that keep to these rules, and one draw needn't show every extreme that they name: Every sequence has at least one valid cache position and some sequence has 128; in each serving group the lengths sum to 16384. `routes`: each row names two different experts; among the rows of one index of tok (aligned blocks of 32 rows) no expert is named by more than 24 rows, and some expert reaches 24 in some block.
All inputs are finite; a program needn't handle non-finite values.
Results may differ from a plain program's by a relative error of at most 0.0075.
Values may be sent and summed in bfloat16 or wider, within the bound.
No kernel may reach another device: no remote copies, remote signals or barrier semaphores. Data moves between devices by JAX's collectives and lax.ppermute only.
A program may use at most 128 MiB of HBM per device.

v0:
```python
import math
import jax
import jax.numpy as jnp
from jax import lax
from jax.sharding import PartitionSpec as P

CAP = 24


def attend(queries, key_new, value_new, cache_keys, cache_values, lengths):
    seq_count, head_count, head_width = queries.shape
    kv_count = key_new.shape[1]
    places = cache_keys.shape[2]
    scaling = 1.0 / math.sqrt(head_width)
    grouped = queries.reshape(seq_count, kv_count, head_count // kv_count, head_width)
    scores = (
        jnp.einsum("skgd,skpd->skgp", grouped, cache_keys, preferred_element_type=jnp.float32)
        * scaling
    )
    usable = jnp.arange(places, dtype=jnp.int32)[None, :] < lengths[:, None]
    scores = jnp.where(usable[:, None, None, :], scores, -jnp.inf)
    own_score = (
        jnp.einsum("skgd,skd->skg", grouped, key_new, preferred_element_type=jnp.float32) * scaling
    )
    top_score = jnp.maximum(jnp.max(scores, axis=-1), own_score)
    weights = jnp.exp(scores - top_score[..., None])
    own_weight = jnp.exp(own_score - top_score)
    totals = jnp.sum(weights, axis=-1) + own_weight
    prob_low = (weights / totals[..., None]).astype(jnp.bfloat16)
    own_low = (own_weight / totals).astype(jnp.bfloat16)
    mixture = jnp.einsum(
        "skgp,skpd->skgd", prob_low, cache_values, preferred_element_type=jnp.float32
    )
    mixture = (
        mixture
        + own_low.astype(jnp.float32)[..., None] * value_new.astype(jnp.float32)[:, :, None, :]
    )
    return mixture.astype(jnp.bfloat16).reshape(seq_count, head_count * head_width)


def gating(normed, chosen, router_weight):
    logits = jnp.dot(normed.astype(jnp.float32), router_weight, precision=lax.Precision.HIGHEST)
    expert_ids = jnp.arange(router_weight.shape[1], dtype=jnp.int32)
    picks = (chosen[:, :, None] == expert_ids[None, None, :]).astype(jnp.float32)
    chosen_logits = jnp.sum(picks * logits[:, None, :], axis=-1)
    leading = jax.nn.sigmoid(chosen_logits[:, 0] - chosen_logits[:, 1])
    gates = jnp.stack([leading, 1.0 - leading], axis=1)
    return (gates, picks)


def expert_rows(block, gate_weight, up_weight, down_weight):
    gated = jnp.dot(block, gate_weight, preferred_element_type=jnp.float32)
    upward = jnp.dot(block, up_weight, preferred_element_type=jnp.float32)
    active = (jax.nn.silu(gated) * upward).astype(jnp.bfloat16)
    return jnp.dot(active, down_weight, preferred_element_type=jnp.float32)


def local(
    hidden_in,
    queries,
    key_new,
    value_new,
    cache_keys,
    cache_values,
    lengths,
    out_weight,
    norm_gain,
    router_weight,
    gate_weight,
    up_weight,
    down_weight,
    routes,
):
    seq_rows = hidden_in.shape[0]
    model_width = hidden_in.shape[1]
    tok_count = lax.axis_size("tok")
    expert_total = router_weight.shape[1]
    replicas = tok_count // expert_total
    pieces = 1
    rows_each = seq_rows // pieces
    capacity = min(CAP, rows_each)
    first_row = lax.axis_index("tok") * seq_rows
    attn_out = attend(queries, key_new, value_new, cache_keys, cache_values, lengths)
    columns = jnp.dot(
        lax.all_gather(attn_out, "tok", axis=0, tiled=True),
        out_weight,
        preferred_element_type=jnp.float32,
    )
    partial_out = lax.all_to_all(columns, "tok", split_axis=0, concat_axis=1, tiled=True)
    projected = lax.psum(partial_out, "side")
    stream = (hidden_in.astype(jnp.float32) + projected).astype(jnp.bfloat16).astype(jnp.float32)
    normed = (
        stream * lax.rsqrt(jnp.mean(stream * stream, axis=-1, keepdims=True) + 1e-05) * norm_gain
    ).astype(jnp.bfloat16)
    chosen = lax.dynamic_slice_in_dim(routes, first_row + 0, rows_each, 0)
    gates, picks = gating(normed, chosen, router_weight)
    hits = jnp.sum(picks, axis=1)
    ranks = jnp.cumsum(hits, axis=0) - hits
    slot_ids = jnp.arange(capacity, dtype=jnp.float32)
    placed = hits[:, :, None] * (ranks[:, :, None] == slot_ids[None, None, :]).astype(jnp.float32)
    send_rows = jnp.einsum(
        "bec,bd->ecd", placed.astype(jnp.bfloat16), normed, preferred_element_type=jnp.float32
    ).astype(jnp.bfloat16)
    outgoing = jnp.repeat(send_rows, replicas, axis=0)
    arrived = lax.all_to_all(outgoing, "tok", split_axis=0, concat_axis=0, tiled=True)
    sources, slots, width_in = arrived.shape
    partial_rows = expert_rows(
        arrived.reshape(sources * slots, width_in), gate_weight, up_weight, down_weight
    )
    returned = lax.all_to_all(
        partial_rows.reshape(sources, slots, width_in),
        "tok",
        split_axis=0,
        concat_axis=0,
        tiled=True,
    )
    per_expert = jnp.sum(returned.reshape(expert_total, replicas, capacity, model_width), axis=1)
    slot_gates = (
        jnp.einsum("bk,bke->be", gates, picks, precision=lax.Precision.HIGHEST)[:, :, None] * placed
    )
    combined = jnp.einsum("bec,ecd->bd", slot_gates, per_expert, precision=lax.Precision.HIGHEST)
    combined_all = lax.psum(combined, "side")
    results = (stream + combined_all).astype(jnp.bfloat16)
    return results


def solution(mesh):
    return jax.shard_map(
        local,
        mesh=mesh,
        in_specs=(
            P(("grp", "tok"), None),
            P(("grp", "tok"), "side", None),
            P(("grp", "tok"), "side", None),
            P(("grp", "tok"), "side", None),
            P(("grp", "tok"), "side", None, None),
            P(("grp", "tok"), "side", None, None),
            P(("grp", "tok")),
            P("side", "tok"),
            P(),
            P(),
            P(None, ("tok", "side")),
            P(None, ("tok", "side")),
            P(("tok", "side"), None),
            P("grp", None),
        ),
        out_specs=P(("grp", "tok"), None),
        check_vma=False,
    )
```

profile of v0, /device:TPU:0, one launch (start us, length us, event | category | flops | bytes accessed | tf_op | source)
XLA Modules:
  0.0 225.7 jit_solution(1218781161953350367)
XLA Ops:
  6.5 0.9 iota_compare_fusion.2
  7.4 0.7 convert_element_type.48
  8.2 1.1 fusion.10
  9.3 2.3 %fusion.31 = (f32[32,2,6]{2,1,0:T(2,128)S(1)}, f32[32,2,6,128]{3,2,1,0:T(8,128)S(1)}) fusion(bf16[32,2,128,128]{3,2,1,0:T(8,128)(2,1)S(1)} %copy-done, bf16[32,2,6,128]{3,0,2,1:T(8,128)(2,1)} %bitcast.37, pred[32,128]{1,0:T(8,128)(4,1)S(1)} %iota_compare_fusion.2), kind=kOutput, calls=%fused_computation.57 | convolution fusion | flops 12729984 | bytes 2397696 | tf_op jit(solution)/shard_map/skgd,skpd->skgp/dot_general | solution.py:17
  11.7 0.3 fusion.8
  12.0 0.7 fusion.2
  12.7 0.1 reshape.65
  12.9 33.8 %all_gather.3 = bf16[256,1536]{1,0:T(8,128)(2,1)S(1)} all-gather(bf16[32,1536]{1,0:T(8,128)(2,1)S(1)} %reshape.65), channel_id=1, replica_groups=mesh['grp'=2,'tok'=8,'side'=2] {'tok'}, dimensions={0}, use_global_device_ids=true | all-gather | bytes 884736 | tf_op jit(solution)/shard_map/all_gather | solution.py:85
  46.7 0.6 fusion.32
  47.3 14.9 %all_to_all.29 = f32[8,32,384]{2,1,0:T(8,128)S(1)} all-to-all(f32[8,32,384]{2,1,0:T(8,128)S(1)} %bitcast.32), channel_id=1, replica_groups=mesh['grp'=2,'tok'=8,'side'=2] {'tok'}, dimensions={0} | all-to-all | bytes 786432 | tf_op jit(solution)/shard_map/all_to_all | solution.py:89
  62.2 0.8 copy.45
  63.2 16.9 %all-reduce.3.cloned.1.call-done = f32[32,3072]{1,0:T(8,128)} async-done(((f32[32,3072]{1,0:T(8,128)}), f32[32,3072]{1,0:T(8,128)}) %all-reduce.3.cloned.1.call-update) | async-done | bytes 393232 | tf_op jit(solution)/shard_map/psum | solution.py:90
  80.1 1.2 fusion.4
  81.3 0.3 fusion.16
  82.0 0.4 convolution_convert_fusion
  82.3 0.1 broadcast_in_dim.16
  82.5 34.9 %all_to_all.30 = bf16[8,24,3072]{2,1,0:T(8,128)(2,1)S(1)} all-to-all(bf16[8,24,3072]{2,1,0:T(8,128)(2,1)S(1)} %bitcast.29), channel_id=1, replica_groups=mesh['grp'=2,'tok'=8,'side'=2] {'tok'}, dimensions={0} | all-to-all | bytes 2359296 | tf_op jit(solution)/shard_map/all_to_all | solution.py:105
  117.4 8.4 %fusion.33 = f32[192,2048]{1,0:T(8,128)} fusion(bf16[192,3072]{1,0:T(8,128)(2,1)S(1)} %bitcast.34, bf16[3072,2048]{1,0:T(8,128)(2,1)} %param.24), kind=kOutput, calls=%fused_computation.59 | convolution fusion | flops 2415919104 | bytes 15335424 | tf_op jit(solution)/shard_map/dot_general | solution.py:52
  125.8 15.3 %fusion.3 = f32[192,3072]{1,0:T(8,128)} fusion(bf16[2048,3072]{1,0:T(8,128)(2,1)} %param.26, bf16[192,3072]{1,0:T(8,128)(2,1)S(1)} %bitcast.35, bf16[3072,2048]{1,0:T(8,128)(2,1)} %param.25, f32[192,2048]{1,0:T(8,128)} %fusion.33), kind=kOutput, calls=%fused_computation.9 | convolution fusion | flops 4834197504 | bytes 30277632 | tf_op jit(solution)/shard_map/dot_general | solution.py:55
  141.1 57.0 %all_to_all.31 = f32[8,24,3072]{2,1,0:T(8,128)S(1)} all-to-all(f32[8,24,3072]{2,1,0:T(8,128)} %bitcast.30), channel_id=1, replica_groups=mesh['grp'=2,'tok'=8,'side'=2] {'tok'}, dimensions={0} | all-to-all | bytes 4718592 | tf_op jit(solution)/shard_map/all_to_all | solution.py:110
  198.1 0.1 bitcast_reduce_fusion
  198.3 1.5 convolution_bitcast_fusion
  199.7 17.5 %all-reduce.5.cloned.1.call-done = f32[32,3072]{1,0:T(8,128)} async-done(((f32[32,3072]{1,0:T(8,128)}), f32[32,3072]{1,0:T(8,128)}) %all-reduce.5.cloned.1.call-update) | async-done | bytes 393232 | tf_op jit(solution)/shard_map/psum | solution.py:122
  217.2 1.7 fusion.7
  (30 shorter events, 0.6 us)
Async XLA Ops:
  6.5 2.7 %copy-start = (bf16[32,2,128,128]{3,2,1,0:T(8,128)(2,1)S(1)}, bf16[32,2,128,128]{3,2,1,0:T(8,128)(2,1)}, u32[]{:S(2)}) copy-start(bf16[32,2,128,128]{3,2,1,0:T(8,128)(2,1)} %param.18) | copy-start | bytes 6291460
  6.5 73.6 %all-reduce.3.cloned.1.call-start = ((), (), s32[]{:S(2)}) async-start(), calls=%async_computation.3 | async-start | bytes 786432 | tf_op jit(solution)/shard_map/psum | solution.py:90
  9.3 2.7 %copy-start.5 = (bf16[32,2,128,128]{3,2,1,0:T(8,128)(2,1)S(1)}, bf16[32,2,128,128]{3,2,1,0:T(8,128)(2,1)}, u32[]{:S(2)}) copy-start(bf16[32,2,128,128]{3,2,1,0:T(8,128)(2,1)} %param.19) | copy-start | bytes 6291460
  12.0 34.7 %copy-start.1 = (bf16[1536,384]{1,0:T(8,128)(2,1)S(1)}, bf16[1536,384]{1,0:T(8,128)(2,1)}, u32[]{:S(2)}) copy-start(bf16[1536,384]{1,0:T(8,128)(2,1)} %param.21) | copy-start | bytes 3538948
  47.2 15.8 %copy-start.4 = (s32[256,2]{0,1:T(2,128)S(1)}, s32[256,2]{0,1:T(2,128)}, u32[]{:S(2)}) copy-start(s32[256,2]{0,1:T(2,128)} %param.27) | copy-start | bytes 6148
  47.3 32.9 %copy-start.2 = (bf16[32,3072]{1,0:T(8,128)(2,1)S(1)}, bf16[32,3072]{1,0:T(8,128)(2,1)}, u32[]{:S(2)}) copy-start(bf16[32,3072]{1,0:T(8,128)(2,1)} %param.14) | copy-start | bytes 589828
  47.3 34.0 %copy-start.3 = (f32[3072]{0:T(1024)S(1)}, f32[3072]{0:T(1024)}, u32[]{:S(2)}) copy-start(f32[3072]{0:T(1024)} %param.22) | copy-start | bytes 36868
  47.3 34.0 %copy-start.6 = (f32[3072,4]{0,1:T(4,128)S(1)}, f32[3072,4]{0,1:T(4,128)}, u32[]{:S(2)}) copy-start(f32[3072,4]{0,1:T(4,128)} %param.23) | copy-start | bytes 147460
  63.0 154.2 %all-reduce.5.cloned.1.call-start = ((), (), s32[]{:S(2)}) async-start(), calls=%async_computation.4 | async-start | bytes 786432 | tf_op jit(solution)/shard_map/psum | solution.py:122
Sparse Core Ops, SparseCore 0:
  63.1 16.9 all-reduce.2
  199.9 17.2 all-reduce.4
where the time goes:
time: 226 us
  blocking collectives  141 us (62%)
  waiting for transfers between devices  34.4 us (15%)
  matrix products  30.5 us (13%)
  between operations  13.6 us (6%)
  other arithmetic  5.14 us (2%)
    all_to_all x1, blocking collectives, local(): lax.all_to_all(partial_rows.reshape(sources, slots, width_in), 'tok', spl...  57 us
    all_to_all x1, blocking collectives, local(): lax.all_to_all(outgoing, 'tok', split_axis=0, concat_axis=0, tiled=True)  34.9 us
    all_gather x1, blocking collectives, local(): lax.all_gather(attn_out, 'tok', axis=0, tiled=True)  33.8 us
    psum x1, waiting for transfers between devices, local(): combined_all = lax.psum(combined, 'side')  17.5 us
    psum x1, waiting for transfers between devices, local(): projected = lax.psum(partial_out, 'side')  16.9 us
    dot_general x1, matrix products, expert_rows(): return jnp.dot(active, down_weight, preferred_element_type=jnp.float32)  15.3 us
    all_to_all x1, blocking collectives, local(): lax.all_to_all(columns, 'tok', split_axis=0, concat_axis=1, tiled=True)  14.9 us
    dot_general x1, matrix products, expert_rows(): gated = jnp.dot(block, gate_weight, preferred_element_type=jnp.float32)  8.39 us
  transfers between devices with their start and end apart: 2, of which 2 were waited for; matrix products, arithmetic and copies ran while one was open for 0% of the time, Pallas kernels for 0%

commit v1 on v0

--- a/solution.py
+++ b/solution.py
@@ -87,7 +87,7 @@
         preferred_element_type=jnp.float32,
     )
     partial_out = lax.all_to_all(columns, "tok", split_axis=0, concat_axis=1, tiled=True)
-    projected = lax.psum(partial_out, "side")
+    projected = jnp.sum(lax.all_gather(partial_out, "side"), axis=0)
     stream = (hidden_in.astype(jnp.float32) + projected).astype(jnp.bfloat16).astype(jnp.float32)
     normed = (
         stream * lax.rsqrt(jnp.mean(stream * stream, axis=-1, keepdims=True) + 1e-05) * norm_gain

time: 226 us -> 208 us (0.920)
  blocking collectives: 141 us -> 126 us
  waiting for transfers between devices: 34.4 us -> 26.5 us
  starting transfers between devices: 0.04 us -> 5.53 us
    psum x1 -> x0, waiting for transfers between devices: 16.9 us -> none  [local(): projected = lax.psum(partial_out, 'side')]
    all_to_all x1 -> x0, blocking collectives: 14.9 us -> none  [local(): lax.all_to_all(columns, 'tok', split_axis=0, concat_axis=1, tiled=True)]
    all_to_all x0 -> x1, waiting for transfers between devices: none -> 9.07 us  [local(): lax.all_to_all(columns, 'tok', split_axis=0, concat_axis=1, tiled=True)]
    all_to_all x0 -> x1, starting transfers between devices: none -> 5.49 us  [local(): lax.all_to_all(columns, 'tok', split_axis=0, concat_axis=1, tiled=True)]
    all_to_all x1, blocking collectives: 34.9 us -> 32.4 us  [local(): lax.all_to_all(outgoing, 'tok', split_axis=0, concat_axis=0, tiled=True)]
    all_gather x0 -> x1, blocking collectives: none -> 2.5 us  [local(): projected = jnp.sum(lax.all_gather(partial_out, 'side'), axis=0)]
where the time goes in v1:
time: 208 us
  blocking collectives  126 us (61%)
  matrix products  31.2 us (15%)
  waiting for transfers between devices  26.5 us (13%)
  between operations  13.6 us (7%)
  starting transfers between devices  5.53 us (3%)
  other arithmetic  4.18 us (2%)
    all_to_all x1, blocking collectives, local(): lax.all_to_all(partial_rows.reshape(sources, slots, width_in), 'tok', spl...  57 us
    all_gather x1, blocking collectives, local(): lax.all_gather(attn_out, 'tok', axis=0, tiled=True)  33.9 us
    all_to_all x1, blocking collectives, local(): lax.all_to_all(outgoing, 'tok', split_axis=0, concat_axis=0, tiled=True)  32.4 us
    psum x1, waiting for transfers between devices, local(): combined_all = lax.psum(combined, 'side')  17.4 us
    dot_general x1, matrix products, expert_rows(): return jnp.dot(active, down_weight, preferred_element_type=jnp.float32)  15.2 us
    all_to_all x1, waiting for transfers between devices, local(): lax.all_to_all(columns, 'tok', split_axis=0, concat_axis=1, tiled=True)  9.07 us
    dot_general x1, matrix products, expert_rows(): gated = jnp.dot(block, gate_weight, preferred_element_type=jnp.float32)  8.34 us
    all_to_all x1, starting transfers between devices, local(): lax.all_to_all(columns, 'tok', split_axis=0, concat_axis=1, tiled=True)  5.49 us
  transfers between devices with their start and end apart: 2, of which 2 were waited for; matrix products, arithmetic and copies ran while one was open for 0% of the time, Pallas kernels for 0%

profile of v1, /device:TPU:0, one launch (start us, length us, event | category | flops | bytes accessed | tf_op | source)
XLA Modules:
  0.0 207.6 jit_solution(12459570026214497629)
XLA Ops:
  6.5 0.9 iota_compare_fusion.2
  7.4 0.7 convert_element_type.48
  8.1 1.1 fusion.10
  9.3 2.3 %fusion.31 = (f32[32,2,6]{2,1,0:T(2,128)S(1)}, f32[32,2,6,128]{3,2,1,0:T(8,128)S(1)}) fusion(bf16[32,2,128,128]{3,2,1,0:T(8,128)(2,1)S(1)} %copy-done, bf16[32,2,6,128]{3,0,2,1:T(8,128)(2,1)} %bitcast.33, pred[32,128]{1,0:T(8,128)(4,1)S(1)} %iota_compare_fusion.2), kind=kOutput, calls=%fused_computation.57 | convolution fusion | flops 12729984 | bytes 2397696 | tf_op jit(solution)/shard_map/skgd,skpd->skgp/dot_general | solution.py:17
  11.7 0.3 fusion.8
  12.0 0.7 fusion.2
  12.7 0.1 reshape.66
  12.9 33.9 %all_gather.9 = bf16[256,1536]{1,0:T(8,128)(2,1)S(1)} all-gather(bf16[32,1536]{1,0:T(8,128)(2,1)S(1)} %reshape.66), channel_id=1, replica_groups=mesh['grp'=2,'tok'=8,'side'=2] {'tok'}, dimensions={0}, use_global_device_ids=true | all-gather | bytes 884736 | tf_op jit(solution)/shard_map/all_gather | solution.py:85
  46.8 1.3 fusion.32
  48.1 5.5 %all-to-all-start = ((f32[8,32,384]{2,1,0:T(8,128)}), f32[8,32,384]{2,1,0:T(8,128)S(1)}, u32[]{:S(2)}, u32[]{:S(2)}) async-start(f32[8,32,384]{2,1,0:T(8,128)} %bitcast.4), calls=%async_computation | async-start | bytes 786432 | tf_op jit(solution)/shard_map/all_to_all | solution.py:89
  53.7 9.1 %all-to-all-done = f32[8,32,384]{2,1,0:T(8,128)S(1)} async-done(((f32[8,32,384]{2,1,0:T(8,128)}), f32[8,32,384]{2,1,0:T(8,128)S(1)}, u32[]{:S(2)}, u32[]{:S(2)}) %all-to-all-start) | async-done | bytes 393248 | tf_op jit(solution)/shard_map/all_to_all | solution.py:89
  62.8 0.2 copy.33
  63.1 2.5 %all_gather.11 = f32[2,32,3072]{2,1,0:T(8,128)S(1)} all-gather(f32[1,32,3072]{2,1,0:T(8,128)S(1)} %all_gather.10), channel_id=1, replica_groups=mesh['grp'=2,'tok'=8,'side'=2] {'side'}, dimensions={0}, use_global_device_ids=true | all-gather | bytes 1179648 | tf_op jit(solution)/shard_map/all_gather | solution.py:90
  65.7 0.2 fusion.4
  65.9 0.3 fusion.16
  66.5 0.4 convolution_convert_fusion
  67.1 32.4 %all_to_all.26 = bf16[8,24,3072]{2,1,0:T(8,128)(2,1)S(1)} all-to-all(bf16[8,24,3072]{2,1,0:T(8,128)(2,1)S(1)} %bitcast.27), channel_id=1, replica_groups=mesh['grp'=2,'tok'=8,'side'=2] {'tok'}, dimensions={0} | all-to-all | bytes 2359296 | tf_op jit(solution)/shard_map/all_to_all | solution.py:105
  99.4 8.3 %fusion.33 = f32[192,2048]{1,0:T(8,128)} fusion(bf16[192,3072]{1,0:T(8,128)(2,1)S(1)} %bitcast.30, bf16[3072,2048]{1,0:T(8,128)(2,1)} %param.24), kind=kOutput, calls=%fused_computation.59 | convolution fusion | flops 2415919104 | bytes 15335424 | tf_op jit(solution)/shard_map/dot_general | solution.py:52
  107.8 15.2 %fusion.3 = f32[192,3072]{1,0:T(8,128)} fusion(bf16[2048,3072]{1,0:T(8,128)(2,1)} %param.26, bf16[192,3072]{1,0:T(8,128)(2,1)S(1)} %bitcast.31, bf16[3072,2048]{1,0:T(8,128)(2,1)} %param.25, f32[192,2048]{1,0:T(8,128)} %fusion.33), kind=kOutput, calls=%fused_computation.9 | convolution fusion | flops 4834197504 | bytes 30277632 | tf_op jit(solution)/shard_map/dot_general | solution.py:55
  123.0 57.0 %all_to_all.27 = f32[8,24,3072]{2,1,0:T(8,128)S(1)} all-to-all(f32[8,24,3072]{2,1,0:T(8,128)} %bitcast.28), channel_id=1, replica_groups=mesh['grp'=2,'tok'=8,'side'=2] {'tok'}, dimensions={0} | all-to-all | bytes 4718592 | tf_op jit(solution)/shard_map/all_to_all | solution.py:110
  180.0 0.1 bitcast_reduce_fusion
  180.2 1.5 convolution_bitcast_fusion
  181.6 17.4 %all-reduce.2.cloned.1.call-done = f32[32,3072]{1,0:T(8,128)} async-done(((f32[32,3072]{1,0:T(8,128)}), f32[32,3072]{1,0:T(8,128)}) %all-reduce.2.cloned.1.call-update) | async-done | bytes 393232 | tf_op jit(solution)/shard_map/psum | solution.py:122
  199.1 1.7 fusion.7
  (31 shorter events, 0.8 us)
Async XLA Ops:
  6.5 2.7 %copy-start = (bf16[32,2,128,128]{3,2,1,0:T(8,128)(2,1)S(1)}, bf16[32,2,128,128]{3,2,1,0:T(8,128)(2,1)}, u32[]{:S(2)}) copy-start(bf16[32,2,128,128]{3,2,1,0:T(8,128)(2,1)} %param.18) | copy-start | bytes 6291460
  9.3 2.7 %copy-start.5 = (bf16[32,2,128,128]{3,2,1,0:T(8,128)(2,1)S(1)}, bf16[32,2,128,128]{3,2,1,0:T(8,128)(2,1)}, u32[]{:S(2)}) copy-start(bf16[32,2,128,128]{3,2,1,0:T(8,128)(2,1)} %param.19) | copy-start | bytes 6291460
  12.0 34.7 %copy-start.1 = (bf16[1536,384]{1,0:T(8,128)(2,1)S(1)}, bf16[1536,384]{1,0:T(8,128)(2,1)}, u32[]{:S(2)}) copy-start(bf16[1536,384]{1,0:T(8,128)(2,1)} %param.21) | copy-start | bytes 3538948
  46.8 6.9 %copy-start.4 = (s32[256,2]{0,1:T(2,128)S(1)}, s32[256,2]{0,1:T(2,128)}, u32[]{:S(2)}) copy-start(s32[256,2]{0,1:T(2,128)} %param.27) | copy-start | bytes 6148
  48.1 14.7 %all-to-all-start = ((f32[8,32,384]{2,1,0:T(8,128)}), f32[8,32,384]{2,1,0:T(8,128)S(1)}, u32[]{:S(2)}, u32[]{:S(2)}) async-start(f32[8,32,384]{2,1,0:T(8,128)} %bitcast.4), calls=%async_computation | async-start | bytes 786432 | tf_op jit(solution)/shard_map/all_to_all | solution.py:89
  53.6 145.5 %all-reduce.2.cloned.1.call-start = ((), (), s32[]{:S(2)}) async-start(), calls=%async_computation.3 | async-start | bytes 786432 | tf_op jit(solution)/shard_map/psum | solution.py:122
  63.0 2.7 %copy-start.2 = (bf16[32,3072]{1,0:T(8,128)(2,1)S(1)}, bf16[32,3072]{1,0:T(8,128)(2,1)}, u32[]{:S(2)}) copy-start(bf16[32,3072]{1,0:T(8,128)(2,1)} %param.14) | copy-start | bytes 589828
  63.1 2.8 %copy-start.3 = (f32[3072]{0:T(1024)S(1)}, f32[3072]{0:T(1024)}, u32[]{:S(2)}) copy-start(f32[3072]{0:T(1024)} %param.22) | copy-start | bytes 36868
  63.1 2.8 %copy-start.6 = (f32[3072,4]{0,1:T(4,128)S(1)}, f32[3072,4]{0,1:T(4,128)}, u32[]{:S(2)}) copy-start(f32[3072,4]{0,1:T(4,128)} %param.23) | copy-start | bytes 147460
Sparse Core Ops, SparseCore 0:
  181.8 17.2 all-reduce.1
